TPU v7x, 32 devices: a whole 2x2x4 slice. The times are simulated.
32 devices in a mesh: dp: 8 (over z, x), cand: 4 (over y, core).
Axes of the slice: x: 2, y: 2, z: 4, core: 2. Of those that a mesh axis runs over, the one named last changes fastest.
Arguments:
- hidden: bfloat16 [16, 32, 128, 768], P('dp', 'cand'), may hold values from -24 to 24
- attn_weight: bfloat16 [768, 3072], P('dp'), may hold values from -1 to 1
- norm_gain: float32 [768], replicated, may hold values from 0.2 to 4
- pos_bias: float32 [12, 128, 128], replicated, may hold values from -5 to 5
- score_weight: float32 [768], replicated, may hold values from -4 to 4
- pair_lengths: int32 [16, 32], P('dp', 'cand'), may hold values from 32 to 128
- labels: int32 [16, 32], P('dp', 'cand'), may hold values from 0 to 3
Outputs:
- update: float32 [768, 3072], P('dp')
- loss: float32 [16], P('dp')
All inputs are finite; a program needn't handle non-finite values.
Results may differ from a plain program's by a relative error of at most 0.017.
Values may be sent and summed in bfloat16 or wider, within the bound.
No kernel may reach another device: no remote copies, remote signals or barrier semaphores. Data moves between devices by JAX's collectives and lax.ppermute only.
A program may use at most 128 MiB of HBM per device.

v0:
```python
import jax
import jax.numpy as jnp
from jax import lax
from jax.sharding import PartitionSpec as P

EPS = 1e-06


def rms_rows(values, gain):
    factor = lax.rsqrt(jnp.mean(values * values, axis=-1, keepdims=True) + EPS)
    return values * factor * gain


def attend(qkv, pos_bias, pair_len):
    batch, seq, triple = qkv.shape
    width = triple // 3
    heads = pos_bias.shape[0]
    head_size = width // heads
    parts = qkv.reshape(batch, seq, 3, heads, head_size)
    logits = jnp.einsum(
        "bqhd,bkhd->bhqk", parts[:, :, 0], parts[:, :, 1], preferred_element_type=jnp.float32
    )
    logits = logits + pos_bias[None]
    valid = jnp.arange(seq, dtype=jnp.int32)[None, :] < pair_len[:, None]
    logits = jnp.where(valid[:, None, None, :], logits, -1e30)
    highest = jnp.max(logits, axis=-1, keepdims=True)
    expo = jnp.exp(logits - highest)
    probs = (expo / jnp.sum(expo, axis=-1, keepdims=True)).astype(jnp.bfloat16)
    context = jnp.einsum(
        "bhqk,bkhd->bqhd", probs, parts[:, :, 2], preferred_element_type=jnp.float32
    )
    return context.astype(jnp.bfloat16).reshape(batch, seq, width)


def score_head(pooled, score_weight):
    return jnp.sum(rms_rows(pooled, 1.0) * score_weight, axis=-1)


def shards(hidden, attn_weight, norm_gain, pos_bias, score_weight, pair_lengths, labels):
    q_local, c_local, seq, width = hidden.shape
    weights = lax.all_gather(attn_weight, "dp", axis=0, tiled=True)
    tokens = hidden.reshape(q_local * c_local, seq, width)
    pair_len = pair_lengths.reshape(-1)
    values = tokens.astype(jnp.float32)
    normed = rms_rows(values, norm_gain).astype(jnp.bfloat16)
    flat_norm = normed.reshape(-1, width)
    qkv = jnp.dot(flat_norm, weights[:, : 3 * width], preferred_element_type=jnp.float32)
    qkv = qkv.astype(jnp.bfloat16).reshape(q_local * c_local, seq, 3 * width)
    context, attend_back = jax.vjp(lambda block: attend(block, pos_bias, pair_len), qkv)
    flat_ctx = context.reshape(-1, width)
    out_rows = values + jnp.dot(
        flat_ctx, weights[:, 3 * width :], preferred_element_type=jnp.float32
    ).reshape(values.shape)
    live = (jnp.arange(seq, dtype=jnp.int32)[None, :] < pair_len[:, None]).astype(jnp.float32)
    share = live / pair_len.astype(jnp.float32)[:, None]
    pooled = jnp.sum(out_rows * share[:, :, None], axis=1)
    flat_scores, head_back = jax.vjp(lambda vector: score_head(vector, score_weight), pooled)
    scores = flat_scores.reshape(q_local, c_local)
    target = jnp.exp(labels.astype(jnp.float32))
    highest = lax.pmax(jnp.max(scores, axis=1), "cand")
    expsum, target_sum, target_dot = lax.psum(
        (
            jnp.sum(jnp.exp(scores - highest[:, None]), axis=1),
            jnp.sum(target, axis=1),
            jnp.sum(target * scores, axis=1),
        ),
        "cand",
    )
    loss = highest + jnp.log(expsum) - target_dot / target_sum
    score_grad = jnp.exp(scores - highest[:, None]) / expsum[:, None] - target / target_sum[:, None]
    pooled_grad = head_back(score_grad.reshape(-1))[0]
    out_grad = (pooled_grad[:, None, :] * share[:, :, None]).astype(jnp.bfloat16)
    flat_out = out_grad.reshape(-1, width)
    context_grad = jnp.dot(flat_out, weights[:, 3 * width :].T, preferred_element_type=jnp.float32)
    context_grad = context_grad.astype(jnp.bfloat16).reshape(context.shape)
    qkv_grad = attend_back(context_grad)[0].reshape(-1, 3 * width)
    dims = (((0,), (0,)), ((), ()))
    first = lax.dot_general(flat_norm, qkv_grad, dims, preferred_element_type=jnp.float32)
    second = lax.dot_general(flat_ctx, flat_out, dims, preferred_element_type=jnp.float32)
    shard = lax.psum_scatter(
        jnp.concatenate([first, second], axis=1).astype(jnp.bfloat16),
        "dp",
        scatter_dimension=0,
        tiled=True,
    ).astype(jnp.float32)
    shard = lax.psum(shard.astype(jnp.bfloat16), "cand").astype(jnp.float32)
    squares = lax.psum(jnp.sum(shard * shard), "dp")
    rms_value = jnp.sqrt(squares / (4.0 * width * width))
    update = shard / (rms_value + EPS)
    return (update, loss)


def solution(mesh):
    in_specs = (
        P("dp", "cand", None, None),
        P("dp", None),
        P(),
        P(),
        P(),
        P("dp", "cand"),
        P("dp", "cand"),
    )
    out_specs = (P("dp", None), P("dp"))
    return jax.shard_map(shards, mesh=mesh, in_specs=in_specs, out_specs=out_specs, check_vma=False)
```

profile of v0, /device:TPU:0, one launch (start us, length us, event | category | flops | bytes accessed | tf_op | source)
XLA Modules:
  0.0 460.7 jit_solution(10536083495842605806)
XLA Ops:
  11.3 2.6 multiply_reduce_fusion
  13.9 2.5 multiply_convert_fusion.1
  16.4 2.4 fusion.13
  18.8 73.4 %all-gather.2.cloned.1.call-done = bf16[768,3072]{1,0:T(8,128)(2,1)} async-done(((bf16[96,3072]{1,0:T(8,128)(2,1)}), bf16[768,3072]{1,0:T(8,128)(2,1)}) %all-gather.2.cloned.1.call-update) | async-done | bytes 4718608 | tf_op jit(solution)/shard_map/all_gather | solution.py:41
  92.3 12.5 %convolution_convert_fusion = bf16[2048,2304]{1,0:T(8,128)(2,1)} fusion(bf16[2048,768]{1,0:T(8,128)(2,1)} %fusion.13, bf16[768,3072]{1,0:T(8,128)(2,1)} %all-gather.2.cloned.1.call-done), kind=kOutput, calls=%fused_computation.11 | convolution fusion | flops 7252475904 | bytes 16121856 | tf_op jit(solution)/shard_map/dot_general | solution.py:47
  104.8 12.7 %copy.20 = bf16[2048,2304]{0,1:T(8,128)(2,1)} copy(bf16[2048,2304]{1,0:T(8,128)(2,1)} %convolution_convert_fusion) | data formatting | bytes 18874368 | tf_op jit(solution)/shard_map/convert_element_type | solution.py:48
  117.5 10.9 %copy.45 = bf16[288,8,16,128]{3,2,1,0:T(8,128)(2,1)} copy(bf16[288,8,16,128]{3,1,2,0:T(8,128)(2,1)} %bitcast.104) | data formatting | bytes 18874368
  128.4 6.4 %fusion.56 = (bf16[16,128,1,12,64]{1,0,4,3,2:T(8,128)(2,1)}, bf16[16,128,1,12,64]{1,0,4,3,2:T(8,128)(2,1)}, bf16[16,128,1,12,64]{1,0,4,3,2:T(8,128)(2,1)S(1)}) fusion(bf16[16,128,3,12,64]{1,0,4,3,2:T(8,128)(2,1)} %bitcast.103), kind=kLoop, calls=%fused_computation.91 | loop fusion | bytes 18874368 | tf_op jit(solution)/shard_map/jvp()/slice | solution.py:30
  134.8 7.5 %fusion.5 = (f32[16,12,128]{2,1,0:T(8,128)S(1)}, f32[16,12,128,128]{2,3,1,0:T(8,128)S(1)}) fusion(f32[12,128,128]{1,2,0:T(8,128)S(1)} %copy-done.11, pred[16,128]{1,0:T(8,128)(4,1)S(1)} %iota_compare_fusion, bf16[16,128,1,12,64]{1,0,4,3,2:T(8,128)(2,1)S(1)} %get-tuple-element.15, bf16[16,128,1,12,64]{1,0,4,3,2:T(8,128)(2,1)} %get-tuple-element.14), kind=kOutput, calls=%fused_computation.13 | convolution fusion | flops 412065792 | bytes 19761152 | tf_op jit(solution)/shard_map/jvp(bqhd,bkhd->bhqk)/dot_general | solution.py:20
  142.3 3.4 fusion.37
  146.9 8.1 %convert_reduce_fusion = (f32[16,12,128]{2,1,0:T(8,128)S(1)}, pred[16,12,128,128]{2,3,1,0:T(32,128)(4,1)}, bf16[16,12,128,128]{2,3,1,0:T(8,128)(2,1)S(1)}) fusion(f32[16,12,128]{2,1,0:T(8,128)S(1)} %get-tuple-element.20, f32[16,12,128,128]{2,3,1,0:T(8,128)S(1)} %get-tuple-element.21, f32[12,128,128]{1,2,0:T(8,128)S(1)} %copy-done.11, ...), kind=kLoop, calls=%fused_computation.7 | loop fusion | flops 25141248 | bytes 23103488 | tf_op jit(solution)/shard_map/jvp()/reduce_sum | solution.py:26
  155.0 2.7 fusion.36
  159.2 4.6 fusion.15
  164.3 5.7 %pmax.7 = f32[2]{0:T(128)S(1)} all-reduce(f32[2]{0:T(128)S(1)} %reduce_max.19), channel_id=1, replica_groups=mesh['dp'=8,'cand'=4] {'cand'}, use_global_device_ids=true, to_apply=%region_7.8 | all-reduce | flops 2 | bytes 16 | tf_op jit(solution)/shard_map/pmax | solution.py:60
  170.2 6.6 %all-reduce.3 = (f32[2]{0:T(128)S(1)}, f32[2]{0:T(128)S(1)}, f32[2]{0:T(128)S(1)}) all-reduce(f32[2]{0:T(128)S(1)} %get-tuple-element.3, f32[2]{0:T(128)S(1)} %get-tuple-element.4, f32[2]{0:T(128)S(1)} %get-tuple-element.2), channel_id=1, replica_groups=mesh['dp'=8,'cand'=4] {'cand'}, use_global_device_ids=true, to_apply=%region_11.12 | all-reduce | flops 6 | bytes 48 | tf_op jit(solution)/shard_map/psum | solution.py:61
  177.7 5.3 %convolution_convert_fusion.2 = bf16[2048,768]{1,0:T(8,128)(2,1)} fusion(bf16[2048,768]{1,0:T(8,128)(2,1)S(1)} %fusion.11, bf16[768,3072]{1,0:T(8,128)(2,1)} %all-gather.2.cloned.1.call-done), kind=kOutput, calls=%fused_computation.41 | convolution fusion | flops 2417491968 | bytes 7471104 | tf_op jit(solution)/shard_map/dot_general | solution.py:74
  182.9 4.7 %copy.27 = bf16[2048,768]{0,1:T(8,128)(2,1)} copy(bf16[2048,768]{1,0:T(8,128)(2,1)} %convolution_convert_fusion.2) | data formatting | bytes 6291456 | tf_op jit(solution)/shard_map/convert_element_type | solution.py:75
  187.7 2.9 copy.46
  192.2 9.0 %convert_bitcast_fusion.2 = bf16[16,128,1,12,64]{1,4,3,0,2:T(8,128)(2,1)} fusion(bf16[16,12,128,128]{2,3,1,0:T(8,128)(2,1)} %copy-done.2, bf16[16,12,64,128]{3,0,2,1:T(8,128)(2,1)S(1)} %bitcast.108), kind=kOutput, calls=%fused_computation.50 | convolution fusion | flops 404226048 | bytes 12582912 | tf_op jit(solution)/shard_map/transpose(jvp(bhqk,bkhd->bqhd))/dot_general | solution.py:29
  201.2 12.6 %fusion.3 = (f32[16,12,128]{2,1,0:T(8,128)S(1)}, bf16[16,12,128,128]{2,3,1,0:T(8,128)(2,1)}) fusion(f32[16,12,128]{2,1,0:T(8,128)S(1)} %multiply_divide_fusion, f32[16,12,128]{2,1,0:T(8,128)S(1)} %get-tuple-element.20, f32[16,12,128,128]{2,3,1,0:T(8,128)} %copy-done, f32[12,128,128]{1,2,0:T(8,128)S(1)} %copy-done.11, ...), kind=kOutput, calls=%fused_computation.5 | convolution fusion | flops 427794432 | bytes 26249216 | tf_op jit(solution)/shard_map/transpose(jvp(bhqk,bkhd->bqhd))/dot_general | solution.py:29
  213.9 10.1 %fusion.53 = (f32[16,12,128]{2,1,0:T(8,128)S(1)}, f32[16,12,128,128]{2,3,1,0:T(8,128)}) fusion(f32[16,12,128]{2,1,0:T(8,128)S(1)} %get-tuple-element.20, f32[16,12,128,128]{2,3,1,0:T(8,128)S(1)} %bitcast.102, f32[12,128,128]{1,2,0:T(8,128)S(1)} %copy-done.11, pred[16,128]{1,0:T(8,128)(4,1)S(1)} %iota_compare_fusion, f32[16,12,128]{2,1,0:T(8,128)S(1)} %neg.9, ...), kind=kLoop, calls=%fused_computation.90 | loop fusion | flops 25141248 | bytes 32638976 | tf_op jit(solution)/shard_map/transpose(jvp())/reduce_sum | solution.py:27
  224.1 11.4 %convert_bitcast_fusion.1 = bf16[16,128,1,12,64]{1,4,3,0,2:T(8,128)(2,1)} fusion(bf16[16,128,1,12,64]{1,0,4,3,2:T(8,128)(2,1)} %get-tuple-element.14, f32[16,12,128,128]{2,3,1,0:T(8,128)} %get-tuple-element.9, pred[16,12,128,128]{2,3,1,0:T(32,128)(4,1)} %get-tuple-element.11, f32[16,12,128]{2,1,0:T(8,128)S(1)} %negate_divide_fusion, ...), kind=kOutput, calls=%fused_computation.49 | convolution fusion | flops 413663232 | bytes 22120448 | tf_op jit(solution)/shard_map/transpose(jvp(bqhd,bkhd->bhqk))/dot_general | solution.py:20
  237.0 4.2 convert_bitcast_fusion
  244.2 6.8 %pad_add_fusion = bf16[16,128,3,12,64]{1,4,3,0,2:T(8,128)(2,1)} fusion(bf16[16,128,1,12,64]{1,4,3,0,2:T(8,128)(2,1)} %convert_bitcast_fusion, bf16[16,128,1,12,64]{1,4,3,0,2:T(8,128)(2,1)} %convert_bitcast_fusion.1, bf16[16,128,1,12,64]{1,4,3,0,2:T(8,128)(2,1)S(1)} %copy-done.12), kind=kLoop, calls=%fused_computation.17 | loop fusion | flops 9437184 | bytes 18874368 | tf_op jit(solution)/shard_map/transpose(jvp())/add_any | solution.py:21
  251.0 26.1 %copy.33 = bf16[16,128,3,12,64]{1,0,4,3,2:T(8,128)(2,1)} copy(bf16[16,128,3,12,64]{1,4,3,0,2:T(8,128)(2,1)} %pad_add_fusion) | data formatting | bytes 18874368 | tf_op jit(solution)/shard_map/transpose(jvp())/add_any | solution.py:21
  277.2 2.4 copy.34
  279.6 11.4 %fusion.22 = bf16[768,2304]{1,0:T(8,128)(2,1)S(1)} fusion(bf16[2048,768]{1,0:T(8,128)(2,1)S(1)} %bitcast.113, bf16[288,8,16,128]{3,2,1,0:T(8,128)(2,1)} %bitcast.110), kind=kOutput, calls=%fused_computation.37 | convolution fusion | flops 7249526784 | bytes 16121856 | tf_op jit(solution)/shard_map/dot_general | solution.py:78
  291.0 2.6 fusion.38
  293.7 2.8 pad_maximum_fusion
  296.5 94.1 %reduce-scatter.2.cloned.1.call-done = bf16[96,3072]{1,0:T(8,128)(2,1)} async-done(((bf16[768,3072]{1,0:T(8,128)(2,1)}), bf16[96,3072]{1,0:T(8,128)(2,1)}) %reduce-scatter.2.cloned.1.call-update) | async-done | bytes 589840 | tf_op jit(solution)/shard_map/reduce_scatter | solution.py:80
  390.6 35.8 %all-reduce.6.cloned.1.call-done = bf16[96,3072]{1,0:T(8,128)(2,1)} async-done(((bf16[96,3072]{1,0:T(8,128)(2,1)}), bf16[96,3072]{1,0:T(8,128)(2,1)}) %all-reduce.6.cloned.1.call-update) | async-done | bytes 589840 | tf_op jit(solution)/shard_map/psum | solution.py:86
  428.9 22.0 %psum.38 = f32[]{:T(128)} all-reduce(f32[]{:T(128)} %fusion.41), channel_id=1, replica_groups=mesh['dp'=8,'cand'=4] {'dp'}, use_global_device_ids=true, to_apply=%region_19.20 | all-reduce | flops 1 | bytes 8 | tf_op jit(solution)/shard_map/psum | solution.py:87
  (76 shorter events, 19.3 us)
Async XLA Ops:
  7.2 6.8 %copy-start.5 = (bf16[2,8,128,768]{3,2,1,0:T(8,128)(2,1)S(1)}, bf16[2,8,128,768]{3,2,1,0:T(8,128)(2,1)}, u32[]{:S(2)}) copy-start(bf16[2,8,128,768]{3,2,1,0:T(8,128)(2,1)} %param.7) | copy-start | bytes 9437188
  7.2 6.8 %copy-start.17 = (f32[768]{0:T(1024)S(1)}, f32[768]{0:T(1024)}, u32[]{:S(2)}) copy-start(f32[768]{0:T(1024)} %param.9) | copy-start | bytes 9220
  7.2 85.1 %all-gather.2.cloned.1.call-start = ((), (), s32[]{:S(2)}) async-start(), calls=%async_computation.1 | async-start | bytes 5308416 | tf_op jit(solution)/shard_map/all_gather | solution.py:41
  7.9 382.7 %reduce-scatter.2.cloned.1.call-start = ((), (), s32[]{:S(2)}) async-start(), calls=%async_computation.2 | async-start | bytes 5308416 | tf_op jit(solution)/shard_map/reduce_scatter | solution.py:80
  128.4 6.4 %copy-start.11 = (f32[12,128,128]{1,2,0:T(8,128)S(1)}, f32[12,128,128]{1,2,0:T(8,128)}, u32[]{:S(2)}) copy-start(f32[12,128,128]{1,2,0:T(8,128)} %copy.24) | copy-start | bytes 2359300
  134.8 7.6 %copy-start.3 = (bf16[16,128,1,12,64]{1,0,4,3,2:T(8,128)(2,1)}, bf16[16,128,1,12,64]{1,0,4,3,2:T(8,128)(2,1)S(1)}, u32[]{:S(2)}) copy-start(bf16[16,128,1,12,64]{1,0,4,3,2:T(8,128)(2,1)S(1)} %get-tuple-element.15) | copy-start | bytes 9437188
  142.3 4.6 copy-start
  146.9 8.1 %copy-start.8 = (bf16[16,128,1,12,64]{1,0,4,3,2:T(8,128)(2,1)S(1)}, bf16[16,128,1,12,64]{1,0,4,3,2:T(8,128)(2,1)}, u32[]{:S(2)}) copy-start(bf16[16,128,1,12,64]{1,0,4,3,2:T(8,128)(2,1)} %get-tuple-element.13) | copy-start | bytes 9437188
  155.0 3.2 copy-start.2
  155.0 4.2 copy-start.6
  158.2 5.6 %copy-start.9 = (bf16[16,12,64,128]{3,2,1,0:T(8,128)(2,1)}, bf16[16,12,64,128]{3,2,1,0:T(8,128)(2,1)S(1)}, u32[]{:S(2)}) copy-start(bf16[16,12,64,128]{3,2,1,0:T(8,128)(2,1)S(1)} %fusion.36) | copy-start | bytes 9437188
  159.2 4.7 %copy-start.16 = (f32[768]{0:T(1024)S(1)}, f32[768]{0:T(1024)}, u32[]{:S(2)}) copy-start(f32[768]{0:T(1024)} %param.11) | copy-start | bytes 9220
  159.2 10.8 %copy-start.18 = (s32[2,8]{1,0:T(2,128)S(1)}, s32[2,8]{1,0:T(2,128)}, u32[]{:S(2)}) copy-start(s32[2,8]{1,0:T(2,128)} %param.13) | copy-start | bytes 196
  190.5 1.6 copy-start.13
  192.2 21.7 %slice-start = ((s8[12582912]{0:T(1024)(128)(4,1)}), s8[4194304]{0:T(1024)(128)(4,1)S(1)}, s32[]{:S(2)}) async-start(s8[12582912]{0:T(1024)(128)(4,1)} %bitcast.101), calls=%async_computation.4 | async-start | bytes 8388608
  201.2 12.7 %slice-start.1 = ((s8[12582912]{0:T(1024)(128)(4,1)}), s8[4194304]{0:T(1024)(128)(4,1)S(1)}, s32[]{:S(2)}) async-start(s8[12582912]{0:T(1024)(128)(4,1)} %bitcast.101), calls=%async_computation.5 | async-start | bytes 8388608
  201.2 12.7 %slice-start.2 = ((s8[12582912]{0:T(1024)(128)(4,1)}), s8[4194304]{0:T(1024)(128)(4,1)S(1)}, s32[]{:S(2)}) async-start(s8[12582912]{0:T(1024)(128)(4,1)} %bitcast.101), calls=%async_computation.6 | async-start | bytes 8388608
  224.1 11.4 %copy-start.1 = (f32[16,12,128,128]{2,3,1,0:T(8,128)S(1)}, f32[16,12,128,128]{2,3,1,0:T(8,128)}, u32[]{:S(2)}) copy-start(f32[16,12,128,128]{2,3,1,0:T(8,128)} %get-tuple-element.9) | copy-start | bytes 37748740
  224.1 11.8 %copy-start.4 = (bf16[16,128,1,12,64]{1,0,4,3,2:T(8,128)(2,1)S(1)}, bf16[16,128,1,12,64]{1,0,4,3,2:T(8,128)(2,1)}, u32[]{:S(2)}) copy-start(bf16[16,128,1,12,64]{1,0,4,3,2:T(8,128)(2,1)} %copy-done.3) | copy-start | bytes 9437188
  224.1 12.9 %copy-start.7 = (pred[16,12,128,128]{2,3,1,0:T(32,128)(4,1)S(1)}, pred[16,12,128,128]{2,3,1,0:T(32,128)(4,1)}, u32[]{:S(2)}) copy-start(pred[16,12,128,128]{2,3,1,0:T(32,128)(4,1)} %get-tuple-element.11) | copy-start | bytes 9437188
  241.2 3.0 copy-start.12
  251.0 26.2 %copy-start.10 = (bf16[16,12,64,128]{3,2,1,0:T(8,128)(2,1)S(1)}, bf16[16,12,64,128]{3,2,1,0:T(8,128)(2,1)}, u32[]{:S(2)}) copy-start(bf16[16,12,64,128]{3,2,1,0:T(8,128)(2,1)} %copy-done.9) | copy-start | bytes 9437188
  277.2 2.5 copy-start.15
  279.6 11.4 %copy-start.14 = (bf16[16,128,768]{2,1,0:T(8,128)(2,1)S(1)}, bf16[16,128,768]{2,1,0:T(8,128)(2,1)}, u32[]{:S(2)}) copy-start(bf16[16,128,768]{2,1,0:T(8,128)(2,1)} %multiply_convert_fusion) | copy-start | bytes 9437188
  296.5 130.0 %all-reduce.6.cloned.1.call-start = ((), (), s32[]{:S(2)}) async-start(), calls=%async_computation.3 | async-start | bytes 1179648 | tf_op jit(solution)/shard_map/psum | solution.py:86
Sparse Core Ops, SparseCore 0:
  10.2 82.0 all-gather.1
  296.6 93.9 reduce-scatter.1
  393.0 33.3 all-reduce.5
where the time goes:
time: 464 us; the launch traced here: 461 us
  waiting for transfers between devices  204 us (44%)
  matrix products  83.9 us (18%)
  local copies, waits for them, and re-layouts  76.2 us (16%)
  other arithmetic  47.1 us (10%)
  blocking collectives  34.2 us (7%)
  between operations  15.2 us (3%)
    reduce_scatter x1, waiting for transfers between devices, shards(): lax.psum_scatter(jnp.concatenate([first, second], axis=1).astype(jnp.bflo...  94.1 us
    all_gather x1, waiting for transfers between devices, shards(): weights = lax.all_gather(attn_weight, 'dp', axis=0, tiled=True)  73.4 us
    psum x1, waiting for transfers between devices, shards(): shard = lax.psum(shard.astype(jnp.bfloat16), 'cand').astype(jnp.float32)  35.8 us
    add_any x1, local copies, waits for them, and re-layouts, attend(): parts[:, :, 0]  26.1 us
    dot_general x3, matrix products, attend(): jnp.einsum('bhqk,bkhd->bqhd', probs, parts[:, :, 2], preferred_element_ty...  24.4 us
    dot_general x3, matrix products, attend(): jnp.einsum('bqhd,bkhd->bhqk', parts[:, :, 0], parts[:, :, 1], preferred_e...  23.1 us
    unnamed x47, local copies, waits for them, and re-layouts  22.7 us
    psum x1, blocking collectives, shards(): squares = lax.psum(jnp.sum(shard * shard), 'dp')  22 us
  transfers between devices with their start and end apart: 3, of which 3 were waited for; matrix products, arithmetic and copies ran while one was open for 2% of the time, Pallas kernels for 0%

commit v1 on v0

--- a/solution.py
+++ b/solution.py
@@ -83,7 +83,7 @@
         scatter_dimension=0,
         tiled=True,
     ).astype(jnp.float32)
-    shard = lax.psum(shard.astype(jnp.bfloat16), "cand").astype(jnp.float32)
+    shard = jnp.sum(lax.all_gather(shard.astype(jnp.bfloat16), "cand"), axis=0).astype(jnp.float32)
     squares = lax.psum(jnp.sum(shard * shard), "dp")
     rms_value = jnp.sqrt(squares / (4.0 * width * width))
     update = shard / (rms_value + EPS)

time: 464 us -> 454 us (0.978)
  waiting for transfers between devices: 204 us -> 194 us
    psum x1 -> x0, waiting for transfers between devices: 35.8 us -> none  [shards(): shard = lax.psum(shard.astype(jnp.bfloat16), 'cand').astype(jnp.float32)]
    all_gather x0 -> x1, waiting for transfers between devices: none -> 25.3 us  [shards(): lax.all_gather(shard.astype(jnp.bfloat16), 'cand')]
where the time goes in v1:
time: 454 us; the launch traced here: 450 us
  waiting for transfers between devices  194 us (43%)
  matrix products  83.9 us (18%)
  local copies, waits for them, and re-layouts  76.2 us (17%)
  other arithmetic  47.1 us (10%)
  blocking collectives  34.2 us (8%)
  between operations  15.2 us (3%)
    reduce_scatter x1, waiting for transfers between devices, shards(): lax.psum_scatter(jnp.concatenate([first, second], axis=1).astype(jnp.bflo...  94.1 us
    all_gather x1, waiting for transfers between devices, shards(): weights = lax.all_gather(attn_weight, 'dp', axis=0, tiled=True)  73.4 us
    add_any x1, local copies, waits for them, and re-layouts, attend(): parts[:, :, 0]  26.1 us
    all_gather x1, waiting for transfers between devices, shards(): lax.all_gather(shard.astype(jnp.bfloat16), 'cand')  25.3 us
    dot_general x3, matrix products, attend(): jnp.einsum('bhqk,bkhd->bqhd', probs, parts[:, :, 2], preferred_element_ty...  24.4 us
    dot_general x3, matrix products, attend(): jnp.einsum('bqhd,bkhd->bhqk', parts[:, :, 0], parts[:, :, 1], preferred_e...  23.1 us
    unnamed x47, local copies, waits for them, and re-layouts  22.7 us
    psum x1, blocking collectives, shards(): squares = lax.psum(jnp.sum(shard * shard), 'dp')  22 us
  transfers between devices with their start and end apart: 3, of which 3 were waited for; matrix products, arithmetic and copies ran while one was open for 2% of the time, Pallas kernels for 0%

profile of v1, /device:TPU:0, one launch (start us, length us, event | category | flops | bytes accessed | tf_op | source)
XLA Modules:
  0.0 450.2 jit_solution(3799032806727815553)
XLA Ops:
  11.3 2.6 multiply_reduce_fusion
  13.9 2.5 multiply_convert_fusion.1
  16.4 2.4 fusion.13
  18.8 73.4 %all-gather.4.cloned.1.call-done = bf16[768,3072]{1,0:T(8,128)(2,1)} async-done(((bf16[96,3072]{1,0:T(8,128)(2,1)}), bf16[768,3072]{1,0:T(8,128)(2,1)}) %all-gather.4.cloned.1.call-update) | async-done | bytes 4718608 | tf_op jit(solution)/shard_map/all_gather | solution.py:41
  92.3 12.5 %convolution_convert_fusion = bf16[2048,2304]{1,0:T(8,128)(2,1)} fusion(bf16[2048,768]{1,0:T(8,128)(2,1)} %fusion.13, bf16[768,3072]{1,0:T(8,128)(2,1)} %all-gather.4.cloned.1.call-done), kind=kOutput, calls=%fused_computation.11 | convolution fusion | flops 7252475904 | bytes 16121856 | tf_op jit(solution)/shard_map/dot_general | solution.py:47
  104.8 12.7 %copy.20 = bf16[2048,2304]{0,1:T(8,128)(2,1)} copy(bf16[2048,2304]{1,0:T(8,128)(2,1)} %convolution_convert_fusion) | data formatting | bytes 18874368 | tf_op jit(solution)/shard_map/convert_element_type | solution.py:48
  117.5 10.9 %copy.45 = bf16[288,8,16,128]{3,2,1,0:T(8,128)(2,1)} copy(bf16[288,8,16,128]{3,1,2,0:T(8,128)(2,1)} %bitcast.105) | data formatting | bytes 18874368
  128.4 6.4 %fusion.56 = (bf16[16,128,1,12,64]{1,0,4,3,2:T(8,128)(2,1)}, bf16[16,128,1,12,64]{1,0,4,3,2:T(8,128)(2,1)}, bf16[16,128,1,12,64]{1,0,4,3,2:T(8,128)(2,1)S(1)}) fusion(bf16[16,128,3,12,64]{1,0,4,3,2:T(8,128)(2,1)} %bitcast.104), kind=kLoop, calls=%fused_computation.91 | loop fusion | bytes 18874368 | tf_op jit(solution)/shard_map/jvp()/slice | solution.py:30
  134.8 7.5 %fusion.5 = (f32[16,12,128]{2,1,0:T(8,128)S(1)}, f32[16,12,128,128]{2,3,1,0:T(8,128)S(1)}) fusion(f32[12,128,128]{1,2,0:T(8,128)S(1)} %copy-done.11, pred[16,128]{1,0:T(8,128)(4,1)S(1)} %iota_compare_fusion, bf16[16,128,1,12,64]{1,0,4,3,2:T(8,128)(2,1)S(1)} %get-tuple-element.15, bf16[16,128,1,12,64]{1,0,4,3,2:T(8,128)(2,1)} %get-tuple-element.14), kind=kOutput, calls=%fused_computation.13 | convolution fusion | flops 412065792 | bytes 19761152 | tf_op jit(solution)/shard_map/jvp(bqhd,bkhd->bhqk)/dot_general | solution.py:20
  142.3 3.4 fusion.37
  146.9 8.1 %convert_reduce_fusion = (f32[16,12,128]{2,1,0:T(8,128)S(1)}, pred[16,12,128,128]{2,3,1,0:T(32,128)(4,1)}, bf16[16,12,128,128]{2,3,1,0:T(8,128)(2,1)S(1)}) fusion(f32[16,12,128]{2,1,0:T(8,128)S(1)} %get-tuple-element.20, f32[16,12,128,128]{2,3,1,0:T(8,128)S(1)} %get-tuple-element.21, f32[12,128,128]{1,2,0:T(8,128)S(1)} %copy-done.11, ...), kind=kLoop, calls=%fused_computation.7 | loop fusion | flops 25141248 | bytes 23103488 | tf_op jit(solution)/shard_map/jvp()/reduce_sum | solution.py:26
  155.0 2.7 fusion.36
  159.2 4.6 %fusion.15 = f32[16,768]{1,0:T(8,128)S(1)} fusion(f32[16,128]{1,0:T(8,128)S(1)} %get-tuple-element.19, bf16[2,8,128,768]{3,2,1,0:T(8,128)(2,1)S(1)} %copy-done.6, bf16[16,128,768]{1,2,0:T(8,128)(2,1)S(1)} %bitcast.106, bf16[768,3072]{1,0:T(8,128)(2,1)} %all-gather.4.cloned.1.call-done), kind=kOutput, calls=%fused_computation.27 | convolution fusion | flops 2422198272 | bytes 7528448 | tf_op jit(solution)/shard_map/dot_general | solution.py:51
  164.3 5.7 %pmax.7 = f32[2]{0:T(128)S(1)} all-reduce(f32[2]{0:T(128)S(1)} %reduce_max.19), channel_id=1, replica_groups=mesh['dp'=8,'cand'=4] {'cand'}, use_global_device_ids=true, to_apply=%region_7.8 | all-reduce | flops 2 | bytes 16 | tf_op jit(solution)/shard_map/pmax | solution.py:60
  170.2 6.6 %all-reduce.3 = (f32[2]{0:T(128)S(1)}, f32[2]{0:T(128)S(1)}, f32[2]{0:T(128)S(1)}) all-reduce(f32[2]{0:T(128)S(1)} %get-tuple-element.3, f32[2]{0:T(128)S(1)} %get-tuple-element.4, f32[2]{0:T(128)S(1)} %get-tuple-element.2), channel_id=1, replica_groups=mesh['dp'=8,'cand'=4] {'cand'}, use_global_device_ids=true, to_apply=%region_11.12 | all-reduce | flops 6 | bytes 48 | tf_op jit(solution)/shard_map/psum | solution.py:61
  177.7 5.3 %convolution_convert_fusion.2 = bf16[2048,768]{1,0:T(8,128)(2,1)} fusion(bf16[2048,768]{1,0:T(8,128)(2,1)S(1)} %fusion.11, bf16[768,3072]{1,0:T(8,128)(2,1)} %all-gather.4.cloned.1.call-done), kind=kOutput, calls=%fused_computation.41 | convolution fusion | flops 2417491968 | bytes 7471104 | tf_op jit(solution)/shard_map/dot_general | solution.py:74
  182.9 4.7 %copy.27 = bf16[2048,768]{0,1:T(8,128)(2,1)} copy(bf16[2048,768]{1,0:T(8,128)(2,1)} %convolution_convert_fusion.2) | data formatting | bytes 6291456 | tf_op jit(solution)/shard_map/convert_element_type | solution.py:75
  187.7 2.9 copy.46
  192.2 9.0 %convert_bitcast_fusion.2 = bf16[16,128,1,12,64]{1,4,3,0,2:T(8,128)(2,1)} fusion(bf16[16,12,128,128]{2,3,1,0:T(8,128)(2,1)} %copy-done.2, bf16[16,12,64,128]{3,0,2,1:T(8,128)(2,1)S(1)} %bitcast.109), kind=kOutput, calls=%fused_computation.50 | convolution fusion | flops 404226048 | bytes 12582912 | tf_op jit(solution)/shard_map/transpose(jvp(bhqk,bkhd->bqhd))/dot_general | solution.py:29
  201.2 12.6 %fusion.3 = (f32[16,12,128]{2,1,0:T(8,128)S(1)}, bf16[16,12,128,128]{2,3,1,0:T(8,128)(2,1)}) fusion(f32[16,12,128]{2,1,0:T(8,128)S(1)} %multiply_divide_fusion, f32[16,12,128]{2,1,0:T(8,128)S(1)} %get-tuple-element.20, f32[16,12,128,128]{2,3,1,0:T(8,128)} %copy-done, f32[12,128,128]{1,2,0:T(8,128)S(1)} %copy-done.11, ...), kind=kOutput, calls=%fused_computation.5 | convolution fusion | flops 427794432 | bytes 26249216 | tf_op jit(solution)/shard_map/transpose(jvp(bhqk,bkhd->bqhd))/dot_general | solution.py:29
  213.9 10.1 %fusion.53 = (f32[16,12,128]{2,1,0:T(8,128)S(1)}, f32[16,12,128,128]{2,3,1,0:T(8,128)}) fusion(f32[16,12,128]{2,1,0:T(8,128)S(1)} %get-tuple-element.20, f32[16,12,128,128]{2,3,1,0:T(8,128)S(1)} %bitcast.103, f32[12,128,128]{1,2,0:T(8,128)S(1)} %copy-done.11, pred[16,128]{1,0:T(8,128)(4,1)S(1)} %iota_compare_fusion, f32[16,12,128]{2,1,0:T(8,128)S(1)} %neg.9, ...), kind=kLoop, calls=%fused_computation.90 | loop fusion | flops 25141248 | bytes 32638976 | tf_op jit(solution)/shard_map/transpose(jvp())/reduce_sum | solution.py:27
  224.1 11.4 %convert_bitcast_fusion.1 = bf16[16,128,1,12,64]{1,4,3,0,2:T(8,128)(2,1)} fusion(bf16[16,128,1,12,64]{1,0,4,3,2:T(8,128)(2,1)} %get-tuple-element.14, f32[16,12,128,128]{2,3,1,0:T(8,128)} %get-tuple-element.9, pred[16,12,128,128]{2,3,1,0:T(32,128)(4,1)} %get-tuple-element.11, f32[16,12,128]{2,1,0:T(8,128)S(1)} %negate_divide_fusion, ...), kind=kOutput, calls=%fused_computation.49 | convolution fusion | flops 413663232 | bytes 22120448 | tf_op jit(solution)/shard_map/transpose(jvp(bqhd,bkhd->bhqk))/dot_general | solution.py:20
  237.0 4.2 convert_bitcast_fusion
  244.2 6.8 %pad_add_fusion = bf16[16,128,3,12,64]{1,4,3,0,2:T(8,128)(2,1)} fusion(bf16[16,128,1,12,64]{1,4,3,0,2:T(8,128)(2,1)} %convert_bitcast_fusion, bf16[16,128,1,12,64]{1,4,3,0,2:T(8,128)(2,1)} %convert_bitcast_fusion.1, bf16[16,128,1,12,64]{1,4,3,0,2:T(8,128)(2,1)S(1)} %copy-done.12), kind=kLoop, calls=%fused_computation.17 | loop fusion | flops 9437184 | bytes 18874368 | tf_op jit(solution)/shard_map/transpose(jvp())/add_any | solution.py:21
  251.0 26.1 %copy.33 = bf16[16,128,3,12,64]{1,0,4,3,2:T(8,128)(2,1)} copy(bf16[16,128,3,12,64]{1,4,3,0,2:T(8,128)(2,1)} %pad_add_fusion) | data formatting | bytes 18874368 | tf_op jit(solution)/shard_map/transpose(jvp())/add_any | solution.py:21
  277.2 2.4 copy.34
  279.6 11.4 %fusion.22 = bf16[768,2304]{1,0:T(8,128)(2,1)S(1)} fusion(bf16[2048,768]{1,0:T(8,128)(2,1)S(1)} %bitcast.114, bf16[288,8,16,128]{3,2,1,0:T(8,128)(2,1)} %bitcast.111), kind=kOutput, calls=%fused_computation.37 | convolution fusion | flops 7249526784 | bytes 16121856 | tf_op jit(solution)/shard_map/dot_general | solution.py:78
  291.0 2.6 fusion.38
  293.7 2.8 pad_maximum_fusion
  296.5 94.1 %reduce-scatter.2.cloned.1.call-done = bf16[96,3072]{1,0:T(8,128)(2,1)} async-done(((bf16[768,3072]{1,0:T(8,128)(2,1)}), bf16[96,3072]{1,0:T(8,128)(2,1)}) %reduce-scatter.2.cloned.1.call-update) | async-done | bytes 589840 | tf_op jit(solution)/shard_map/reduce_scatter | solution.py:80
  390.6 25.3 %all-gather.6.cloned.1.call-done = bf16[384,3072]{1,0:T(8,128)(2,1)} async-done(((bf16[96,3072]{1,0:T(8,128)(2,1)}), bf16[384,3072]{1,0:T(8,128)(2,1)}) %all-gather.6.cloned.1.call-update) | async-done | bytes 2359312 | tf_op jit(solution)/shard_map/all_gather | solution.py:86
  419.4 22.0 %psum.30 = f32[]{:T(128)} all-reduce(f32[]{:T(128)} %fusion.41), channel_id=1, replica_groups=mesh['dp'=8,'cand'=4] {'dp'}, use_global_device_ids=true, to_apply=%region_19.20 | all-reduce | flops 1 | bytes 8 | tf_op jit(solution)/shard_map/psum | solution.py:87
  (77 shorter events, 19.3 us)
Async XLA Ops:
  7.2 6.8 %copy-start.5 = (bf16[2,8,128,768]{3,2,1,0:T(8,128)(2,1)S(1)}, bf16[2,8,128,768]{3,2,1,0:T(8,128)(2,1)}, u32[]{:S(2)}) copy-start(bf16[2,8,128,768]{3,2,1,0:T(8,128)(2,1)} %param.7) | copy-start | bytes 9437188
  7.2 6.8 %copy-start.17 = (f32[768]{0:T(1024)S(1)}, f32[768]{0:T(1024)}, u32[]{:S(2)}) copy-start(f32[768]{0:T(1024)} %param.9) | copy-start | bytes 9220
  7.2 85.1 %all-gather.4.cloned.1.call-start = ((), (), s32[]{:S(2)}) async-start(), calls=%async_computation.1 | async-start | bytes 5308416 | tf_op jit(solution)/shard_map/all_gather | solution.py:41
  7.9 382.7 %reduce-scatter.2.cloned.1.call-start = ((), (), s32[]{:S(2)}) async-start(), calls=%async_computation.2 | async-start | bytes 5308416 | tf_op jit(solution)/shard_map/reduce_scatter | solution.py:80
  128.4 6.4 %copy-start.11 = (f32[12,128,128]{1,2,0:T(8,128)S(1)}, f32[12,128,128]{1,2,0:T(8,128)}, u32[]{:S(2)}) copy-start(f32[12,128,128]{1,2,0:T(8,128)} %copy.24) | copy-start | bytes 2359300
  134.8 7.6 %copy-start.3 = (bf16[16,128,1,12,64]{1,0,4,3,2:T(8,128)(2,1)}, bf16[16,128,1,12,64]{1,0,4,3,2:T(8,128)(2,1)S(1)}, u32[]{:S(2)}) copy-start(bf16[16,128,1,12,64]{1,0,4,3,2:T(8,128)(2,1)S(1)} %get-tuple-element.15) | copy-start | bytes 9437188
  142.3 4.6 %copy-start = (f32[16,12,128,128]{2,3,1,0:T(8,128)}, f32[16,12,128,128]{2,3,1,0:T(8,128)S(1)}, u32[]{:S(2)}) copy-start(f32[16,12,128,128]{2,3,1,0:T(8,128)S(1)} %get-tuple-element.21) | copy-start | bytes 37748740
  146.9 8.1 %copy-start.8 = (bf16[16,128,1,12,64]{1,0,4,3,2:T(8,128)(2,1)S(1)}, bf16[16,128,1,12,64]{1,0,4,3,2:T(8,128)(2,1)}, u32[]{:S(2)}) copy-start(bf16[16,128,1,12,64]{1,0,4,3,2:T(8,128)(2,1)} %get-tuple-element.13) | copy-start | bytes 9437188
  155.0 3.2 copy-start.2
  155.0 4.2 copy-start.6
  158.2 5.6 %copy-start.9 = (bf16[16,12,64,128]{3,2,1,0:T(8,128)(2,1)}, bf16[16,12,64,128]{3,2,1,0:T(8,128)(2,1)S(1)}, u32[]{:S(2)}) copy-start(bf16[16,12,64,128]{3,2,1,0:T(8,128)(2,1)S(1)} %fusion.36) | copy-start | bytes 9437188
  159.2 4.7 %copy-start.16 = (f32[768]{0:T(1024)S(1)}, f32[768]{0:T(1024)}, u32[]{:S(2)}) copy-start(f32[768]{0:T(1024)} %param.11) | copy-start | bytes 9220
  159.2 10.8 %copy-start.18 = (s32[2,8]{1,0:T(2,128)S(1)}, s32[2,8]{1,0:T(2,128)}, u32[]{:S(2)}) copy-start(s32[2,8]{1,0:T(2,128)} %param.13) | copy-start | bytes 196
  190.5 1.6 copy-start.13
  192.2 21.7 %slice-start = ((s8[12582912]{0:T(1024)(128)(4,1)}), s8[4194304]{0:T(1024)(128)(4,1)S(1)}, s32[]{:S(2)}) async-start(s8[12582912]{0:T(1024)(128)(4,1)} %bitcast.102), calls=%async_computation.4 | async-start | bytes 8388608
  201.2 12.7 %slice-start.1 = ((s8[12582912]{0:T(1024)(128)(4,1)}), s8[4194304]{0:T(1024)(128)(4,1)S(1)}, s32[]{:S(2)}) async-start(s8[12582912]{0:T(1024)(128)(4,1)} %bitcast.102), calls=%async_computation.5 | async-start | bytes 8388608
  201.2 12.7 %slice-start.2 = ((s8[12582912]{0:T(1024)(128)(4,1)}), s8[4194304]{0:T(1024)(128)(4,1)S(1)}, s32[]{:S(2)}) async-start(s8[12582912]{0:T(1024)(128)(4,1)} %bitcast.102), calls=%async_computation.6 | async-start | bytes 8388608
  224.1 11.4 %copy-start.1 = (f32[16,12,128,128]{2,3,1,0:T(8,128)S(1)}, f32[16,12,128,128]{2,3,1,0:T(8,128)}, u32[]{:S(2)}) copy-start(f32[16,12,128,128]{2,3,1,0:T(8,128)} %get-tuple-element.9) | copy-start | bytes 37748740
  224.1 11.8 %copy-start.4 = (bf16[16,128,1,12,64]{1,0,4,3,2:T(8,128)(2,1)S(1)}, bf16[16,128,1,12,64]{1,0,4,3,2:T(8,128)(2,1)}, u32[]{:S(2)}) copy-start(bf16[16,128,1,12,64]{1,0,4,3,2:T(8,128)(2,1)} %copy-done.3) | copy-start | bytes 9437188
  224.1 12.9 %copy-start.7 = (pred[16,12,128,128]{2,3,1,0:T(32,128)(4,1)S(1)}, pred[16,12,128,128]{2,3,1,0:T(32,128)(4,1)}, u32[]{:S(2)}) copy-start(pred[16,12,128,128]{2,3,1,0:T(32,128)(4,1)} %get-tuple-element.11) | copy-start | bytes 9437188
  241.2 3.0 copy-start.12
  251.0 26.2 %copy-start.10 = (bf16[16,12,64,128]{3,2,1,0:T(8,128)(2,1)S(1)}, bf16[16,12,64,128]{3,2,1,0:T(8,128)(2,1)}, u32[]{:S(2)}) copy-start(bf16[16,12,64,128]{3,2,1,0:T(8,128)(2,1)} %copy-done.9) | copy-start | bytes 9437188
  277.2 2.5 copy-start.15
  279.6 11.4 %copy-start.14 = (bf16[16,128,768]{2,1,0:T(8,128)(2,1)S(1)}, bf16[16,128,768]{2,1,0:T(8,128)(2,1)}, u32[]{:S(2)}) copy-start(bf16[16,128,768]{2,1,0:T(8,128)(2,1)} %multiply_convert_fusion) | copy-start | bytes 9437188
  296.5 119.5 %all-gather.6.cloned.1.call-start = ((), (), s32[]{:S(2)}) async-start(), calls=%async_computation.3 | async-start | bytes 2949120 | tf_op jit(solution)/shard_map/all_gather | solution.py:86
Sparse Core Ops, SparseCore 0:
  10.2 82.0 all-gather.3
  296.6 93.9 reduce-scatter.1
  392.2 23.6 all-gather.5
